TPU v7x, 32 devices: a whole 2x2x4 slice. The times are simulated.
32 devices in a mesh: pair: 8 (over z, core), orb: 4 (over y, x).
Axes of the slice: x: 2, y: 2, z: 4, core: 2. Of those that a mesh axis runs over, the one named last changes fastest.
Arguments:
- amplitudes: float32 [128, 128, 128], P(('pair', 'orb')), may hold values from -3 to 3
- couple: int32 [128, 16], P(('pair', 'orb')), may hold values from 0 to 127, as said below
- occ_first: int32 [128], P('pair'), may hold values from 0 to 31, as said below
- occ_second: int32 [128], P('pair'), may hold values from 0 to 31, as said below
- couple_intersection: bfloat16 [128, 16, 128, 128], P(('pair', 'orb')), may hold values from -0.375 to 0.375
- pno_maps: bfloat16 [128, 2, 128, 128], P('pair'), may hold values from -0.5 to 0.5
- orbital_blocks: bfloat16 [32, 512, 128], P('pair', 'orb'), may hold values from -2 to 2
- pno_energy: float32 [128, 128], P(('pair', 'orb')), may hold values from 0.5 to 2.5
- occ_energy: float32 [32], replicated, may hold values from -1.5 to -0.3
Outputs:
- new_amplitudes: float32 [128, 128, 128], P(('pair', 'orb'))
- dressed: float32 [32, 512, 128], P('pair', 'orb')
Inputs may be any that keep to these rules, and one draw needn't show every extreme that they name: `couple`: every listed partner of a pair lies in the same pair group as the pair (pairs g * 16 to (g + 1) * 16 - 1 form group g). `occ_first`: the pairs of group g have first orbitals in g * 4 to (g + 1) * 4 - 1. `occ_second`: the pairs of group g have second orbitals among the orbitals of groups g - 1 to g + 1, counted modulo 8 (group h holds orbitals h * 4 to (h + 1) * 4 - 1).
All inputs are finite; a program needn't handle non-finite values.
Results may differ from a plain program's by a relative error of at most 0.014.
Values may be sent and summed in bfloat16 or wider, within the bound.
A program may use at most 64 MiB of HBM per device.

v0:
```python
import functools

import jax
import jax.numpy as jnp
from jax import lax
from jax.experimental import pallas as pl
from jax.experimental.pallas import tpu as pltpu
from jax.sharding import PartitionSpec as P

REACH = 1
ITERS = 2
SIDES = 2 * REACH + 1

dress_scale = 0.015

NN = (((1,), (0,)), ((), ()))
NT = (((1,), (1,)), ((), ()))


def dot(left, right, dims=NN):
    return lax.dot_general(left, right, dims, preferred_element_type=jnp.float32)


def kernel(
    ranks,
    groups,
    couple_hbm,
    first_hbm,
    second_hbm,
    energy_hbm,
    amps_hbm,
    pno_hbm,
    inter_hbm,
    maps_hbm,
    orb_hbm,
    out_amps,
    out_dressed,
    couple,
    occ_first,
    occ_second,
    occ_energy,
    amplitudes,
    pno_energy,
    inter,
    maps,
    first_t,
    amps_0,
    amps_1,
    window_0,
    window_1,
    second_z,
    parts_out,
    parts_in,
    half,
    fitted,
    amp_send,
    amp_recv,
    win_send,
    win_recv,
    part_send,
    part_recv,
    inter_sem,
    maps_sem,
    orb_sem,
    small_sem,
):
    amps = (amps_0, amps_1)
    window = (window_0, window_1)
    own_pairs = amps_hbm.shape[0]
    orbs = orb_hbm.shape[0]
    partners = couple.shape[1]
    size = amplitudes.shape[2]
    me = lax.axis_index("orb")
    group = lax.axis_index("pair")
    own = me * own_pairs
    own_rows = pl.ds(own, own_pairs)
    middle = pl.ds(REACH * orbs, orbs)
    bf16 = jnp.bfloat16
    square = ranks == 4 and own_pairs % 2 == 0
    low = own_pairs // 2
    lower, upper = pl.ds(0, low), pl.ds(low, own_pairs - low)

    def target(step):
        if square:
            return (me // 2 + step // 2) % 2 * 2 + (me + step) % 2
        return (me + step) % ranks

    def source(step):
        return target(step) if square else (me + ranks - step) % ranks

    orb_copy = pltpu.make_async_copy(orb_hbm, window[0].at[middle], orb_sem)
    orb_copy.start()
    small_copies = [
        pltpu.make_async_copy(source_ref, target_ref, small_sem.at[at])
        for at, (source_ref, target_ref) in enumerate(
            (
                (amps_hbm, amplitudes),
                (couple_hbm, couple),
                (first_hbm, occ_first),
                (second_hbm, occ_second),
                (energy_hbm, occ_energy),
                (pno_hbm, pno_energy),
            )
        )
    ]
    for copy in small_copies:
        copy.start()
    maps_copies = []
    for part in range(2):
        chunk = pl.ds(part * (maps.shape[0] // 2), maps.shape[0] // 2)
        maps_copies.append(
            pltpu.make_async_copy(maps_hbm.at[chunk], maps.at[chunk], maps_sem.at[part])
        )
        maps_copies[-1].start()
    inter_copies = []
    for i in range(own_pairs):
        inter_copies.append(pltpu.make_async_copy(inter_hbm.at[i], inter.at[i], inter_sem.at[i]))
        inter_copies[-1].start()

    barrier = pltpu.get_barrier_semaphore()
    for step in range(1, ranks):
        pl.semaphore_signal(
            barrier,
            inc=1,
            device_id={"orb": (me + step) % ranks},
            device_id_type=pl.DeviceIdType.MESH,
        )
    for step in range(1, REACH + 1):
        for shift in (step, groups - step):
            pl.semaphore_signal(
                barrier,
                inc=1,
                device_id={"pair": (group + shift) % groups},
                device_id_type=pl.DeviceIdType.MESH,
            )
    small_copies[0].wait()
    for i in range(own_pairs):
        amps[0][own + i] = amplitudes[i].astype(bf16)
    pl.semaphore_wait(barrier, ranks - 1 + 2 * REACH)

    def win_copy(turn, place):
        return pltpu.make_async_remote_copy(
            src_ref=window[turn].at[middle],
            dst_ref=window[turn].at[pl.ds(place * orbs, orbs)],
            send_sem=win_send.at[turn, place],
            recv_sem=win_recv.at[turn, place],
            device_id={"pair": (group + REACH - place + groups) % groups},
            device_id_type=pl.DeviceIdType.MESH,
        )

    def amp_copy(turn, step, i):
        return pltpu.make_async_remote_copy(
            src_ref=amps[turn].at[own + i],
            dst_ref=amps[turn].at[own + i],
            send_sem=amp_send.at[turn, step, i],
            recv_sem=amp_recv.at[turn, step, i],
            device_id={"orb": target(step)},
            device_id_type=pl.DeviceIdType.MESH,
        )

    def amp_relay(turn, i):
        via, onto = (1, 2) if i < low else (2, 1)
        place = target(via) * own_pairs + i
        return pltpu.make_async_remote_copy(
            src_ref=amps[turn].at[place],
            dst_ref=amps[turn].at[place],
            send_sem=amp_send.at[turn, 3, i],
            recv_sem=amp_recv.at[turn, 3, i],
            device_id={"orb": target(onto)},
            device_id_type=pl.DeviceIdType.MESH,
        )

    def relay_all(turn):
        for i in range(low):
            for j, via in ((i, 1), (low + i, 2)):
                amp_copy(turn, via, j).wait_recv()
                amp_relay(turn, j).start()

    def amp_wait(turn, step):
        for i in range(own_pairs):
            if not square:
                amp_copy(turn, step, i).wait_recv()
            elif step == 3:
                amp_relay(turn, i).wait_recv()
            elif (i < low) != (step == 1):
                amp_copy(turn, step, i).wait_recv()

    def part_send_to(turn, step, onto, half_of, sem):
        rows = (slice(None), lower, upper)[half_of] if half_of else pl.ds(0, own_pairs)
        return pltpu.make_async_remote_copy(
            src_ref=parts_out.at[turn, step, rows],
            dst_ref=parts_in.at[turn, step, rows],
            send_sem=part_send.at[turn, sem],
            recv_sem=part_recv.at[turn, sem],
            device_id={"orb": target(onto)},
            device_id_type=pl.DeviceIdType.MESH,
        )

    if square:
        part_first = {1: [(1, 1, 1, 0)], 2: [(2, 2, 2, 1)], 3: [(3, 1, 1, 2), (3, 2, 2, 3)]}
        part_second = [(2, 2, 1, 4), (1, 1, 2, 5)]
        part_last = [(1, 1, 1, 0), (2, 2, 2, 1)] + part_second
        part_all = part_last + part_first[3]
        terms = (1, 2)
    else:
        part_first = {step: [(step, step, 0, step)] for step in range(1, ranks)}
        part_second = []
        part_last = part_all = [entry for step in part_first for entry in part_first[step]]
        terms = range(1, ranks)

    def part_forward(turn):
        for arrived, entry in zip((part_first[3] if square else []), part_second):
            part_send_to(turn, *arrived).wait_recv()
            step, _, half_of, _ = entry
            for i in range(low):
                i = i if half_of == 1 else low + i
                total = parts_out[turn, step, i].astype(jnp.float32)
                total += parts_in[turn, 3, i].astype(jnp.float32)
                parts_out[turn, step, i] = total.astype(bf16)
            part_send_to(turn, *entry).start()

    def amp_start(turn, i):
        for step in (1, 2) if square else range(1, ranks):
            amp_copy(turn, step, i).start()

    places = [place for place in range(SIDES) if place != REACH]

    orb_copy.wait()
    for place in places:
        win_copy(0, place).start()
    if square:
        for i in range(own_pairs):
            for step in (1, 2):
                j = i if step == 1 else (i + low) % own_pairs
                amp_copy(0, step, j).start()
    else:
        for i in range(own_pairs):
            amp_start(0, i)

    for copy in maps_copies + small_copies[1:]:
        copy.wait()

    @pl.loop(0, ranks)
    def _(block):
        for i in range(own_pairs):
            first_t[block * own_pairs + i] = maps[block * own_pairs + i, 0].T

    for turn in range(ITERS):
        for place in places:
            win_copy(turn, place).wait_recv()
        if square and turn == 0:
            relay_all(turn)

        @pl.loop(1, ranks + 1)
        def _(ahead):
            step = ranks - ahead
            base = target(step) * own_pairs
            lefts, rights = [], []
            for i in range(own_pairs):
                pair = base + i
                first = REACH * orbs + occ_first[pair] % orbs
                second = occ_second[pair]
                distance = (second // orbs - group + REACH + groups) % groups
                place = jnp.minimum(distance, SIDES - 1)
                lefts.append(dot(first_t[pair], window[turn][first], NT).astype(bf16))
                rights.append(
                    dot(window[turn][place * orbs + second % orbs], maps[pair, 1]).astype(bf16)
                )
            for i in range(own_pairs):
                second_z[base + i] = rights[i]
                parts_out[turn, step, i] = dot(lefts[i], rights[i]).astype(bf16)

            if square:
                for at in part_first:

                    @pl.when(step == at)
                    def _(at=at):
                        for entry in part_first[at]:
                            part_send_to(turn, *entry).start()
            else:

                @pl.when(step > 0)
                def _():
                    part_send_to(turn, step, step, 0, step).start()

        if square and turn > 0:
            relay_all(turn)

        for o in range(orbs):
            fitted[o] = jnp.zeros_like(fitted[o])

        @pl.loop(0, ranks)
        def _(step):
            if square:
                for at in range(1, ranks):

                    @pl.when(step == at)
                    def _(at=at):
                        amp_wait(turn, at)
            else:

                @pl.when(step > 0)
                def _():
                    amp_wait(turn, step)

            base = source(step) * own_pairs
            halves = [
                dot(second_z[base + i], amps[turn][base + i]).astype(bf16)
                for i in range(own_pairs)
            ]
            returned = [dot(halves[i], first_t[base + i]) for i in range(own_pairs)]
            for o in range(orbs):
                total = fitted[o]
                for i in range(own_pairs):
                    weight = (occ_first[base + i] % orbs == o).astype(jnp.float32)
                    total += weight * returned[i]
                fitted[o] = total

        for o in range(orbs):
            value = window[0][REACH * orbs + o].astype(jnp.float32) + dress_scale * fitted[o]
            if turn + 1 < ITERS:
                window[turn + 1][REACH * orbs + o] = value.astype(bf16)
            else:
                out_dressed[o] = value
        if turn + 1 < ITERS:
            for place in places:
                win_copy(turn + 1, place).start()

        part_forward(turn)

        if turn == 0:
            for copy in inter_copies:
                copy.wait()

        @pl.loop(0, own_pairs)
        def _(i):
            for k in range(partners):
                partner = couple[i, k] % (ranks * own_pairs)
                half[i, :, k * size : (k + 1) * size] = dot(
                    inter[i, k], amps[turn][partner]
                ).astype(bf16)
            coupled = None
            for k in range(0, partners, 2):
                right = jnp.concatenate([inter[i, k], inter[i, k + 1]], axis=1)
                term = dot(half[i, :, k * size : (k + 2) * size], right, NT)
                coupled = term if coupled is None else coupled + term

            @pl.when(i == 0)
            def _():
                for entry in part_last:
                    part_send_to(turn, *entry).wait_recv()

            total = parts_out[turn, 0, i].astype(jnp.float32)
            for step in terms:
                total += parts_in[turn, step, i].astype(jnp.float32)
            rows = jnp.broadcast_to(pno_energy[pl.ds(i, 1), :], (size, size))
            denominator = rows + rows.T
            denominator -= occ_energy[occ_first[own + i]]
            denominator -= occ_energy[occ_second[own + i]]
            value = -(total + coupled) / denominator
            if turn + 1 < ITERS:
                amps[turn + 1][own + i] = value.astype(bf16)
                amp_start(turn + 1, i)
            else:
                out_amps[i] = value

    for turn in range(ITERS):
        for place in places:
            win_copy(turn, place).wait_send()
        for entry in part_all:
            part_send_to(turn, *entry).wait_send()
        for i in range(own_pairs):
            for step in range(1, ranks):
                if square and step == 3:
                    amp_relay(turn, i).wait_send()
                else:
                    amp_copy(turn, step, i).wait_send()


def on_device(
    ranks,
    groups,
    amplitudes,
    couple,
    occ_first,
    occ_second,
    couple_intersection,
    pno_maps,
    orbital_blocks,
    pno_energy,
    occ_energy,
):
    own_pairs, size, _ = amplitudes.shape
    group_pairs = occ_first.shape[0]
    orbs, rows, virtuals = orbital_blocks.shape
    partners = couple.shape[1]
    bf16 = jnp.bfloat16
    vmem = pl.BlockSpec(memory_space=pltpu.VMEM)
    hbm = pl.BlockSpec(memory_space=pltpu.HBM)
    dma = pltpu.SemaphoreType.DMA
    return pl.pallas_call(
        functools.partial(kernel, ranks, groups),
        out_shape=(
            pltpu.VMEM(amplitudes.shape, jnp.float32),
            pltpu.VMEM(orbital_blocks.shape, jnp.float32),
        ),
        in_specs=[hbm] * 9,
        out_specs=(vmem, vmem),
        scratch_shapes=[
            pltpu.SMEM(couple.shape, couple.dtype),
            pltpu.SMEM(occ_first.shape, occ_first.dtype),
            pltpu.SMEM(occ_second.shape, occ_second.dtype),
            pltpu.SMEM(occ_energy.shape, occ_energy.dtype),
            pltpu.VMEM(amplitudes.shape, amplitudes.dtype),
            pltpu.VMEM(pno_energy.shape, pno_energy.dtype),
            pltpu.VMEM(couple_intersection.shape, bf16),
            pltpu.VMEM(pno_maps.shape, bf16),
            pltpu.VMEM((group_pairs, size, virtuals), bf16),
            pltpu.VMEM((group_pairs, size, size), bf16),
            pltpu.VMEM((group_pairs, size, size), bf16),
            pltpu.VMEM((SIDES * orbs, rows, virtuals), bf16),
            pltpu.VMEM((SIDES * orbs, rows, virtuals), bf16),
            pltpu.VMEM((group_pairs, rows, size), bf16),
            pltpu.VMEM((ITERS, ranks, own_pairs, size, size), bf16),
            pltpu.VMEM((ITERS, ranks, own_pairs, size, size), bf16),
            pltpu.VMEM((own_pairs, size, partners * size), bf16),
            pltpu.VMEM((orbs, rows, virtuals), jnp.float32),
            dma((ITERS, ranks, own_pairs)),
            dma((ITERS, ranks, own_pairs)),
            dma((ITERS, SIDES)),
            dma((ITERS, SIDES)),
            dma((ITERS, ranks + 2)),
            dma((ITERS, ranks + 2)),
            dma((own_pairs,)),
            dma((2,)),
            dma,
            dma((6,)),
        ],
        compiler_params=pltpu.CompilerParams(
            collective_id=0, has_side_effects=True, vmem_limit_bytes=67043328 - 4096 * 1024
        ),
    )(
        *(pltpu.with_memory_space_constraint(x, pltpu.HBM) for x in (
        couple,
        occ_first,
        occ_second,
        occ_energy,
        amplitudes,
        pno_energy,
        couple_intersection,
        pno_maps,
        orbital_blocks,
        ))
    )


def solution(mesh):
    return jax.shard_map(
        functools.partial(on_device, mesh.shape["orb"], mesh.shape["pair"]),
        mesh=mesh,
        in_specs=(
            P(("pair", "orb"), None, None),
            P(("pair", "orb"), None),
            P("pair"),
            P("pair"),
            P(("pair", "orb"), None, None, None),
            P("pair", None, None, None),
            P("pair", "orb", None),
            P(("pair", "orb"), None),
            P(),
        ),
        out_specs=(P(("pair", "orb"), None, None), P("pair", "orb", None)),
        check_vma=False,
    )
```

profile of v0, /device:TPU:0, one launch (start us, length us, event | category | flops | bytes accessed | tf_op | source)
XLA Modules:
  0.0 35.2 jit_solution(15757355305187622441)
XLA Ops:
  0.6 33.1 %shard_map.104 = (f32[4,128,128]{2,1,0:T(8,128)S(1)}, f32[4,128,128]{2,1,0:T(8,128)S(1)}) custom-call(s32[4,16]{1,0:T(4,128)} %couple_hbm.1, s32[16]{0:T(128)} %first_hbm.1, s32[16]{0:T(128)} %second_hbm.1, f32[32]{0:T(128)} %energy_hbm.1, f32[4,128,128]{2,1,0:T(8,128)} %amps_hbm.1, f32[4,128]{1,0:T(4,128)} %pno_hbm.1, bf16[4,16,128,128]{3,2,1,0:T(8,128)(2,1)} %inter_hbm.1, ...), custom_call_target="tpu_custom_call" | custom-call | tf_op jit(solution)/shard_map/pallas_call | solution.py:401
  33.7 0.7 %copy.13 = f32[4,128,128]{2,1,0:T(8,128)} copy(f32[4,128,128]{2,1,0:T(8,128)S(1)} %get-tuple-element.2) | data formatting | bytes 524288
  34.5 0.7 %copy.14 = f32[4,128,128]{2,1,0:T(8,128)} copy(f32[4,128,128]{2,1,0:T(8,128)S(1)} %get-tuple-element.3) | data formatting | bytes 524288
where the time goes:
time: 35.3 us; the launch traced here: 35.2 us
  Pallas kernels  33.1 us (94%)
  local copies, waits for them, and re-layouts  1.41 us (4%)
  between operations  0.64 us (2%)
    pallas_call x1, Pallas kernels, on_device(): pl.pallas_call(functools.partial(kernel, ranks, groups), out_shape=(pltpu...  33.1 us
    unnamed x2, local copies, waits for them, and re-layouts  1.41 us

commit v1 on v0

v1 whole, which is shorter than its diff:
```python
import functools

import jax
import jax.numpy as jnp
from jax import lax
from jax.experimental import pallas as pl
from jax.experimental.pallas import tpu as pltpu
from jax.sharding import PartitionSpec as P

REACH = 1
ITERS = 2
SIDES = 2 * REACH + 1

dress_scale = 0.015

NN = (((1,), (0,)), ((), ()))
NT = (((1,), (1,)), ((), ()))


def dot(left, right, dims=NN):
    return lax.dot_general(left, right, dims, preferred_element_type=jnp.float32)


def kernel(
    ranks,
    groups,
    couple_hbm,
    first_hbm,
    second_hbm,
    energy_hbm,
    amps_hbm,
    pno_hbm,
    inter_hbm,
    maps_hbm,
    orb_hbm,
    out_amps,
    out_dressed,
    couple,
    occ_first,
    occ_second,
    occ_energy,
    second_at,
    amplitudes,
    pno_energy,
    inter,
    maps,
    first_t,
    blocks_t,
    scale,
    coupled,
    amps_0,
    amps_1,
    window_0,
    window_1,
    parts_out,
    parts_in,
    half,
    fitted,
    amp_send,
    amp_recv,
    win_send,
    win_recv,
    part_send,
    part_recv,
    inter_sem,
    maps_sem,
    orb_sem,
    small_sem,
):
    amps = (amps_0, amps_1)
    window = (window_0, window_1)
    own_pairs = amps_hbm.shape[0]
    orbs = orb_hbm.shape[0]
    partners = couple.shape[1]
    size = amplitudes.shape[2]
    virtuals = orb_hbm.shape[2]
    pairs = ranks * own_pairs
    me = lax.axis_index("orb")
    group = lax.axis_index("pair")
    own = me * own_pairs
    middle = pl.ds(REACH * orbs, orbs)
    places = [place for place in range(SIDES) if place != REACH]
    bf16 = jnp.bfloat16
    square = ranks == 4
    steps = (3, 1, 2) if square else tuple(range(1, ranks))

    def target(step):
        if square:
            return (me // 2 + step // 2) % 2 * 2 + (me + step) % 2
        return (me + step) % ranks

    def source(step):
        return target(step) if square else (me + ranks - step) % ranks

    barrier = pltpu.get_barrier_semaphore()
    for step in range(1, ranks):
        pl.semaphore_signal(
            barrier,
            inc=1,
            device_id={"orb": (me + step) % ranks},
            device_id_type=pl.DeviceIdType.MESH,
        )
    for step in range(1, REACH + 1):
        for shift in (step, groups - step):
            pl.semaphore_signal(
                barrier,
                inc=1,
                device_id={"pair": (group + shift) % groups},
                device_id_type=pl.DeviceIdType.MESH,
            )

    orb_copy = pltpu.make_async_copy(orb_hbm, window[0].at[middle], orb_sem)
    orb_copy.start()
    small_copies = [
        pltpu.make_async_copy(source_ref, target_ref, small_sem.at[at])
        for at, (source_ref, target_ref) in enumerate(
            (
                (amps_hbm, amplitudes),
                (first_hbm, occ_first),
                (second_hbm, occ_second),
                (energy_hbm, occ_energy),
                (pno_hbm, pno_energy),
                (couple_hbm, couple),
            )
        )
    ]
    for copy in small_copies:
        copy.start()
    maps_copy = pltpu.make_async_copy(maps_hbm, maps, maps_sem)
    maps_copy.start()
    inter_copy = pltpu.make_async_copy(inter_hbm, inter, inter_sem)
    inter_copy.start()

    small_copies[0].wait()
    for i in range(own_pairs):
        amps[0][own + i] = amplitudes[i].astype(bf16)
    orb_copy.wait()
    pl.semaphore_wait(barrier, ranks - 1 + 2 * REACH)

    def win_copy(turn, place):
        return pltpu.make_async_remote_copy(
            src_ref=window[turn].at[middle],
            dst_ref=window[turn].at[pl.ds(place * orbs, orbs)],
            send_sem=win_send.at[turn],
            recv_sem=win_recv.at[turn, place],
            device_id={"pair": (group + REACH - place + groups) % groups},
            device_id_type=pl.DeviceIdType.MESH,
        )

    def amp_copy(turn, step, i):
        return pltpu.make_async_remote_copy(
            src_ref=amps[turn].at[own + i],
            dst_ref=amps[turn].at[own + i],
            send_sem=amp_send.at[turn],
            recv_sem=amp_recv.at[turn, step],
            device_id={"orb": target(step)},
            device_id_type=pl.DeviceIdType.MESH,
        )

    def part_copy(turn, step, i):
        return pltpu.make_async_remote_copy(
            src_ref=parts_out.at[turn, i, step],
            dst_ref=parts_in.at[turn, i, step - 1],
            send_sem=part_send.at[turn],
            recv_sem=part_recv.at[turn, i],
            device_id={"orb": target(step)},
            device_id_type=pl.DeviceIdType.MESH,
        )

    def whole(ref, send_sem, recv_sem):
        return pltpu.make_async_remote_copy(
            src_ref=ref,
            dst_ref=ref,
            send_sem=send_sem,
            recv_sem=recv_sem,
            device_id={"orb": target(1)},
            device_id_type=pl.DeviceIdType.MESH,
        )

    def amp_wait(turn, step):
        block = amps[turn].at[pl.ds(source(step) * own_pairs, own_pairs)]
        whole(block, amp_send.at[turn], amp_recv.at[turn, step]).wait_recv()

    def part_wait(turn, i):
        whole(parts_in.at[turn, i], part_send.at[turn], part_recv.at[turn, i]).wait_recv()

    def sent(turn):
        sends = pl.ds(0, (ranks - 1) * own_pairs)
        whole(amps[turn].at[sends], amp_send.at[turn], amp_recv.at[turn, 0]).wait_send()
        sends = pl.ds(0, len(places) * orbs)
        whole(window[turn].at[sends], win_send.at[turn], win_recv.at[turn, 0]).wait_send()

    def parts_sent(turn):
        whole(parts_in.at[turn], part_send.at[turn], part_recv.at[turn, 0]).wait_send()

    def amp_start(turn, i):
        for step in steps:
            amp_copy(turn, step, i).start()

    def win_start(turn):
        for place in places:
            win_copy(turn, place).start()

    def transposed(turn):
        for o in range(orbs):
            blocks_t[o] = window[turn][REACH * orbs + o].T

    def integrals(turn):
        for place in places:
            win_copy(turn, place).wait_recv()

        def one(i):
            for step in steps + (0,):
                pair = target(step) * own_pairs + i
                left = blocks_t[occ_first[pair] % orbs]
                parts_out[turn, i, step] = dot(left, window[turn][second_at[pair]]).astype(bf16)
                if step > 0:
                    part_copy(turn, step, i).start()

        if square:
            for i in range(own_pairs):
                one(i)
        else:
            pl.loop(0, own_pairs)(one)

    def fit(turn, base):
        lefts, rights = [], []
        for i in range(own_pairs):
            pair = base + i
            half_way = dot(maps[pair, 1], amps[turn][pair]).astype(bf16)
            through = dot(half_way, maps[pair, 0], NT)
            local = occ_first[pair] % orbs
            rights.append(
                jnp.concatenate(
                    [jnp.where(local == o, through, 0.0).astype(bf16) for o in range(orbs)], axis=1
                )
            )
            lefts.append(window[turn][second_at[pair]])
        return dot(jnp.concatenate(lefts, axis=1), jnp.concatenate(rights, axis=0))

    def fit_all(turn):
        fitted[...] = fit(turn, own)

        @pl.loop(1, ranks)
        def _(step):
            amp_wait(turn, step)
            fitted[...] += fit(turn, source(step) * own_pairs)

    def dress(turn):
        for o in range(orbs):
            value = window[0][REACH * orbs + o].astype(jnp.float32)
            value += dress_scale * fitted[:, o * virtuals : (o + 1) * virtuals]
            if turn + 1 < ITERS:
                window[turn + 1][REACH * orbs + o] = value.astype(bf16)
            else:
                out_dressed[o] = value

    def couplings(turn, i):
        for k in range(partners):
            partner = couple[i, k] % pairs
            half[:, k * size : (k + 1) * size] = dot(inter[i, k], amps[turn][partner]).astype(bf16)
        total = None
        for k in range(0, partners, 2):
            right = jnp.concatenate([inter[i, k], inter[i, k + 1]], axis=1)
            term = dot(half[:, k * size : (k + 2) * size], right, NT)
            total = term if total is None else total + term
        coupled[i] = total

    def finish(turn, i):
        part_wait(turn, i)
        total = parts_out[turn, i, 0].astype(jnp.float32)
        for step in range(1, ranks):
            total += parts_in[turn, i, step - 1].astype(jnp.float32)
        right = dot(total.astype(bf16), maps[own + i, 1]).astype(bf16)
        value = (dot(first_t[i], right) + coupled[i]) * scale[i]
        if turn + 1 < ITERS:
            amps[turn + 1][own + i] = value.astype(bf16)
            amp_start(turn + 1, i)
        else:
            out_amps[i] = value

    win_start(0)
    for i in range(own_pairs):
        amp_start(0, i)

    for copy in small_copies[1:]:
        copy.wait()

    @pl.loop(0, pairs)
    def _(pair):
        second = occ_second[pair]
        distance = (second // orbs - group + REACH + groups) % groups
        second_at[pair] = jnp.minimum(distance, SIDES - 1) * orbs + second % orbs

    transposed(0)
    maps_copy.wait()
    for i in range(own_pairs):
        first_t[i] = maps[own + i, 0].T
        rows = jnp.broadcast_to(pno_energy[pl.ds(i, 1), :], (size, size))
        denominator = rows + rows.T
        denominator -= occ_energy[occ_first[own + i]]
        denominator -= occ_energy[occ_second[own + i]]
        scale[i] = -1.0 / denominator

    for turn in range(ITERS):
        last = turn + 1 == ITERS
        integrals(turn)
        fit_all(turn)
        dress(turn)
        if not last:
            win_start(turn + 1)
            transposed(turn + 1)
        if turn == 0:
            inter_copy.wait()
        for i in range(own_pairs):
            couplings(turn, i)
        if last:
            sent(turn - 1)
            parts_sent(turn - 1)
        for i in range(own_pairs):
            finish(turn, i)

    sent(ITERS - 1)
    parts_sent(ITERS - 1)


def store(amps, dressed, out_amps, out_dressed, sem):
    copies = [
        pltpu.make_async_copy(amps, out_amps, sem.at[0]),
        pltpu.make_async_copy(dressed, out_dressed, sem.at[1]),
    ]
    for copy in copies:
        copy.start()
    for copy in copies:
        copy.wait()


def on_device(
    ranks,
    groups,
    amplitudes,
    couple,
    occ_first,
    occ_second,
    couple_intersection,
    pno_maps,
    orbital_blocks,
    pno_energy,
    occ_energy,
):
    own_pairs, size, _ = amplitudes.shape
    group_pairs = occ_first.shape[0]
    orbs, rows, virtuals = orbital_blocks.shape
    partners = couple.shape[1]
    bf16 = jnp.bfloat16
    vmem = pl.BlockSpec(memory_space=pltpu.VMEM)
    hbm = pl.BlockSpec(memory_space=pltpu.HBM)
    dma = pltpu.SemaphoreType.DMA
    results = pl.pallas_call(
        functools.partial(kernel, ranks, groups),
        out_shape=(
            pltpu.VMEM(amplitudes.shape, jnp.float32),
            pltpu.VMEM(orbital_blocks.shape, jnp.float32),
        ),
        in_specs=[hbm] * 9,
        out_specs=(vmem, vmem),
        scratch_shapes=[
            pltpu.SMEM(couple.shape, couple.dtype),
            pltpu.SMEM(occ_first.shape, occ_first.dtype),
            pltpu.SMEM(occ_second.shape, occ_second.dtype),
            pltpu.SMEM(occ_energy.shape, occ_energy.dtype),
            pltpu.SMEM(occ_second.shape, occ_second.dtype),
            pltpu.VMEM(amplitudes.shape, amplitudes.dtype),
            pltpu.VMEM(pno_energy.shape, pno_energy.dtype),
            pltpu.VMEM(couple_intersection.shape, bf16),
            pltpu.VMEM(pno_maps.shape, bf16),
            pltpu.VMEM((own_pairs, size, virtuals), bf16),
            pltpu.VMEM((orbs, virtuals, rows), bf16),
            pltpu.VMEM((own_pairs, size, size), jnp.float32),
            pltpu.VMEM((own_pairs, size, size), jnp.float32),
            pltpu.VMEM((group_pairs, size, size), bf16),
            pltpu.VMEM((group_pairs, size, size), bf16),
            pltpu.VMEM((SIDES * orbs, rows, virtuals), bf16),
            pltpu.VMEM((SIDES * orbs, rows, virtuals), bf16),
            pltpu.VMEM((ITERS, own_pairs, ranks, virtuals, virtuals), bf16),
            pltpu.VMEM((ITERS, own_pairs, ranks - 1, virtuals, virtuals), bf16),
            pltpu.VMEM((size, partners * size), bf16),
            pltpu.VMEM((rows, orbs * virtuals), jnp.float32),
            dma((ITERS,)),
            dma((ITERS, ranks)),
            dma((ITERS,)),
            dma((ITERS, SIDES)),
            dma((ITERS,)),
            dma((ITERS, own_pairs)),
            dma,
            dma,
            dma,
            dma((6,)),
        ],
        compiler_params=pltpu.CompilerParams(
            collective_id=0, has_side_effects=True, vmem_limit_bytes=67043328 - 4096 * 1024
        ),
    )(
        *(pltpu.with_memory_space_constraint(x, pltpu.HBM) for x in (
        couple,
        occ_first,
        occ_second,
        occ_energy,
        amplitudes,
        pno_energy,
        couple_intersection,
        pno_maps,
        orbital_blocks,
        ))
    )
    return pl.pallas_call(
        store,
        out_shape=tuple(pltpu.HBM(x.shape, x.dtype) for x in results),
        in_specs=[vmem] * 2,
        out_specs=(hbm, hbm),
        scratch_shapes=[dma((2,))],
        compiler_params=pltpu.CompilerParams(vmem_limit_bytes=4096 * 1024),
    )(*(pltpu.with_memory_space_constraint(x, pltpu.VMEM) for x in results))


def solution(mesh):
    return jax.shard_map(
        functools.partial(on_device, mesh.shape["orb"], mesh.shape["pair"]),
        mesh=mesh,
        in_specs=(
            P(("pair", "orb"), None, None),
            P(("pair", "orb"), None),
            P("pair"),
            P("pair"),
            P(("pair", "orb"), None, None, None),
            P("pair", None, None, None),
            P("pair", "orb", None),
            P(("pair", "orb"), None),
            P(),
        ),
        out_specs=(P(("pair", "orb"), None, None), P("pair", "orb", None)),
        check_vma=False,
    )
```

time: 35.3 us -> 30.9 us (0.88)
  Pallas kernels: 33.1 us -> 30.1 us
  local copies, waits for them, and re-layouts: 1.41 us -> 0 us
    pallas_call x1, Pallas kernels: 33.1 us -> 29.3 us  [on_device(): pl.pallas_call(functools.partial(kernel, ranks, groups), out_shape=(pltpu...]
    unnamed x2 -> x0, local copies, waits for them, and re-layouts: 1.41 us -> none
    pallas_call x0 -> x1, Pallas kernels: none -> 0.81 us  [on_device(): pl.pallas_call(store, out_shape=tuple((pltpu.HBM(x.shape, x.dtype) for x...]
where the time goes in v1:
time: 30.9 us; the launch traced here: 30.8 us
  Pallas kernels  30.1 us (97%)
  between operations  0.64 us (2%)
    pallas_call x1, Pallas kernels, on_device(): pl.pallas_call(functools.partial(kernel, ranks, groups), out_shape=(pltpu...  29.3 us
    pallas_call x1, Pallas kernels, on_device(): pl.pallas_call(store, out_shape=tuple((pltpu.HBM(x.shape, x.dtype) for x...  0.81 us

profile of v1, /device:TPU:0, one launch (start us, length us, event | category | flops | bytes accessed | tf_op | source)
XLA Modules:
  0.0 30.8 jit_solution(17431663339742012867)
XLA Ops:
  0.6 29.3 %shard_map.104 = (f32[4,128,128]{2,1,0:T(8,128)S(1)}, f32[4,128,128]{2,1,0:T(8,128)S(1)}) custom-call(s32[4,16]{1,0:T(4,128)} %couple_hbm.1, s32[16]{0:T(128)} %first_hbm.1, s32[16]{0:T(128)} %second_hbm.1, f32[32]{0:T(128)} %energy_hbm.1, f32[4,128,128]{2,1,0:T(8,128)} %amps_hbm.1, f32[4,128]{1,0:T(4,128)} %pno_hbm.1, bf16[4,16,128,128]{3,2,1,0:T(8,128)(2,1)} %inter_hbm.1, ...), custom_call_target="tpu_custom_call" | custom-call | tf_op jit(solution)/shard_map/pallas_call | solution.py:359
  30.0 0.8 %shard_map.105 = (f32[4,128,128]{2,1,0:T(8,128)}, f32[4,128,128]{2,1,0:T(8,128)}) custom-call(f32[4,128,128]{2,1,0:T(8,128)S(1)} %get-tuple-element.4.amps, f32[4,128,128]{2,1,0:T(8,128)S(1)} %get-tuple-element.5.dressed), custom_call_target="tpu_custom_call" | custom-call | tf_op jit(solution)/shard_map/pallas_call | solution.py:416

commit v2 on v1

v2 whole, which is shorter than its diff:
```python
import functools

import jax
import jax.numpy as jnp
from jax import lax
from jax.experimental import pallas as pl
from jax.experimental.pallas import tpu as pltpu
from jax.sharding import PartitionSpec as P

REACH = 1
ITERS = 2
SIDES = 2 * REACH + 1

dress_scale = 0.015
BATCH = 2

NN = (((1,), (0,)), ((), ()))
NT = (((1,), (1,)), ((), ()))


def dot(left, right, dims=NN):
    return lax.dot_general(left, right, dims, preferred_element_type=jnp.float32)


def kernel(
    ranks,
    groups,
    couple_hbm,
    first_hbm,
    second_hbm,
    energy_hbm,
    amps_hbm,
    pno_hbm,
    inter_hbm,
    maps_hbm,
    orb_hbm,
    out_amps,
    out_dressed,
    couple,
    occ_first,
    occ_second,
    occ_energy,
    second_at,
    amplitudes,
    pno_energy,
    inter,
    inter_t,
    maps,
    first_t,
    blocks_t,
    scale,
    coupled,
    amps,
    amps_now,
    window,
    blocks,
    parts_out,
    parts_in,
    relayed,
    weights,
    fitted,
    amp_send,
    amp_recv,
    win_send,
    win_recv,
    part_send,
    part_recv,
    relay_recv,
    inter_sem,
    maps_sem,
    orb_sem,
    small_sem,
):
    own_pairs = amps_hbm.shape[0]
    orbs = orb_hbm.shape[0]
    partners = couple.shape[1]
    size = amplitudes.shape[2]
    virtuals = orb_hbm.shape[2]
    pairs = ranks * own_pairs
    me = lax.axis_index("orb")
    group = lax.axis_index("pair")
    own = me * own_pairs
    middle = pl.ds(REACH * orbs, orbs)
    places = [place for place in range(SIDES) if place != REACH]
    bf16 = jnp.bfloat16
    square = ranks == 4 and own_pairs % 2 == 0
    z_place = (group + 1) % 2 * 2 * REACH
    c_place = 2 * REACH - z_place

    def target(step):
        if square:
            return (me // 2 + step // 2) % 2 * 2 + (me + step) % 2
        return (me + step) % ranks

    def source(step):
        return target(step) if square else (me + ranks - step) % ranks

    barrier = pltpu.get_barrier_semaphore()
    for step in range(1, ranks):
        pl.semaphore_signal(
            barrier,
            inc=1,
            device_id={"orb": (me + step) % ranks},
            device_id_type=pl.DeviceIdType.MESH,
        )
    for step in range(1, REACH + 1):
        for shift in (step, groups - step):
            pl.semaphore_signal(
                barrier,
                inc=1,
                device_id={"pair": (group + shift) % groups},
                device_id_type=pl.DeviceIdType.MESH,
            )

    small_copies = [
        pltpu.make_async_copy(source_ref, target_ref, small_sem.at[at])
        for at, (source_ref, target_ref) in enumerate(
            (
                (amps_hbm, amplitudes),
                (first_hbm, occ_first),
                (second_hbm, occ_second),
                (energy_hbm, occ_energy),
                (pno_hbm, pno_energy),
                (couple_hbm, couple),
            )
        )
    ]
    small_copies[0].start()
    pl.semaphore_wait(barrier, ranks - 1 + 2 * REACH)

    def win_copy(turn, place, bare=False):
        return pltpu.make_async_remote_copy(
            src_ref=orb_hbm if bare else window.at[turn, middle],
            dst_ref=window.at[turn, pl.ds(place * orbs, orbs)],
            send_sem=win_send.at[turn],
            recv_sem=win_recv.at[turn, place],
            device_id={"pair": (group + REACH - place + groups) % groups},
            device_id_type=pl.DeviceIdType.MESH,
        )

    def amp_copy(turn, step, i):
        return pltpu.make_async_remote_copy(
            src_ref=amps.at[turn, own + i],
            dst_ref=amps.at[turn, own + i],
            send_sem=amp_send.at[turn],
            recv_sem=amp_recv.at[turn, step, i],
            device_id={"orb": target(step)},
            device_id_type=pl.DeviceIdType.MESH,
        )

    def amp_relay(turn, i):
        via, onto = (1, 2) if i % 2 == 0 else (2, 1)
        place = target(via) * own_pairs + i
        return pltpu.make_async_remote_copy(
            src_ref=amps.at[turn, place],
            dst_ref=amps.at[turn, place],
            send_sem=amp_send.at[turn],
            recv_sem=amp_recv.at[turn, 3, i],
            device_id={"orb": target(onto)},
            device_id_type=pl.DeviceIdType.MESH,
        )

    def relay_all(turn):
        for i in range(own_pairs):
            amp_copy(turn, 1 if i % 2 == 0 else 2, i).wait_recv()
            amp_relay(turn, i).start()

    def amp_wait(turn, step):
        for i in range(own_pairs):
            def wait(i=i):
                amp_copy(turn, step, i).wait_recv()

            if not square or step == 3 or (step, i % 2) in ((1, 1), (2, 0)):
                wait()

    def part_copy(turn, step, i):
        return pltpu.make_async_remote_copy(
            src_ref=parts_out.at[turn, i, step],
            dst_ref=parts_in.at[turn, i, step - 1],
            send_sem=part_send.at[turn],
            recv_sem=part_recv.at[turn, i],
            device_id={"orb": target(step)},
            device_id_type=pl.DeviceIdType.MESH,
        )

    def part_relay(turn, i):
        return pltpu.make_async_remote_copy(
            src_ref=parts_out.at[turn, i, 3],
            dst_ref=relayed.at[turn, i],
            send_sem=part_send.at[turn],
            recv_sem=relay_recv.at[turn, i],
            device_id={"orb": target(1 if i % 2 == 0 else 2)},
            device_id_type=pl.DeviceIdType.MESH,
        )

    def forward_all(turn):
        for i in range(own_pairs):
            onto = 2 if i % 2 == 0 else 1
            part_relay(turn, i).wait_recv()
            total = parts_out[turn, i, onto].astype(jnp.float32)
            total += relayed[turn, i].astype(jnp.float32)
            parts_out[turn, i, onto] = total.astype(bf16)
            part_copy(turn, onto, i).start()

    def whole(ref, send_sem, recv_sem):
        return pltpu.make_async_remote_copy(
            src_ref=ref,
            dst_ref=ref,
            send_sem=send_sem,
            recv_sem=recv_sem,
            device_id={"orb": target(1)},
            device_id_type=pl.DeviceIdType.MESH,
        )

    def part_wait(turn, i):
        def wait(terms):
            arrived = parts_in.at[turn, i, pl.ds(0, terms)]
            whole(arrived, part_send.at[turn], part_recv.at[turn, i]).wait_recv()

        wait(2 if square else ranks - 1)

    def sent(turn):
        sends = pl.ds(0, (ranks - 1) * own_pairs)
        whole(amps.at[turn, sends], amp_send.at[turn], amp_recv.at[turn, 0, 0]).wait_send()
        sends = pl.ds(0, len(places) * orbs)
        whole(window.at[turn, sends], win_send.at[turn], win_recv.at[turn, 0]).wait_send()

    def parts_sent(turn):
        whole(parts_in.at[turn], part_send.at[turn], part_recv.at[turn, 0]).wait_send()

    def amp_start(turn, i):
        for step in (1, 2) if square else range(ranks - 1, 0, -1):
            amp_copy(turn, step, i).start()

    def win_start(turn, bare=False):
        win_copy(turn, z_place, bare).start()
        win_copy(turn, c_place, bare).start()

    def transposed(turn):
        for o in range(orbs):
            blocks_t[o] = window[turn, REACH * orbs + o].T

    def integral(turn, step, i):
        pair = target(step) * own_pairs + i
        left = blocks_t[occ_first[pair] % orbs]
        parts_out[turn, i, step] = dot(left, blocks[second_at[pair]]).astype(bf16)

    def integrals(turn):
        for place in places:
            win_copy(turn, place).wait_recv()
        for at in range(SIDES * orbs):
            blocks[at] = window[turn, at]

        def one(i):
            for step in range(ranks - 1, -1, -1):
                integral(turn, step, i)
                if step > 0 and not square:
                    part_copy(turn, step, i).start()

        if square:
            for i in range(own_pairs):
                integral(turn, 3, i)
            for i in range(own_pairs):
                for step in (2, 1, 0):
                    integral(turn, step, i)
        else:
            pl.loop(0, own_pairs)(one)

    def far_sums(turn):
        for i in range(own_pairs):
            part_relay(turn, i).start()

    def near_sums(turn):
        for i in range(own_pairs):
            part_copy(turn, 1 if i % 2 == 0 else 2, i).start()

    def through(turn, step):
        base = source(step) * own_pairs
        halves = []
        for i in range(own_pairs):
            amp = amps[turn, base + i]
            amps_now[base + i] = amp
            halves.append(dot(maps[base + i, 1], amp).astype(bf16))
        wholes = [dot(halves[i], first_t[base + i]) for i in range(own_pairs)]
        for i in range(own_pairs):
            local = occ_first[base + i] % orbs
            rows = pl.ds((step * own_pairs + i) * virtuals, virtuals)
            for o in range(orbs):
                masked = jnp.where(local == o, wholes[i], 0.0).astype(bf16)
                weights[rows, o * virtuals : (o + 1) * virtuals] = masked

    def applied(turn, some):
        lefts = [
            blocks[second_at[source(step) * own_pairs + i]]
            for step in some
            for i in range(own_pairs)
        ]
        rows = own_pairs * virtuals
        right = weights[pl.ds(some[0] * rows, len(some) * rows), :]
        return dot(jnp.concatenate(lefts, axis=1), right)

    def fit_near(turn):
        fitted[...] = applied(turn, near_steps)

    def dress(turn):
        if square:
            total = fitted[...] + applied(turn, far_steps)
        else:

            @pl.loop(1, ranks)
            def _(step):
                fitted[...] += applied(turn, (step,))

            total = fitted[...]
        values = [
            window[0, REACH * orbs + o].astype(jnp.float32)
            + dress_scale * total[:, o * virtuals : (o + 1) * virtuals]
            for o in range(orbs)
        ]

        @pl.when(turn + 1 < ITERS)
        def _():
            for o in range(orbs):
                window[turn + 1, REACH * orbs + o] = values[o].astype(bf16)

        @pl.when(turn + 1 == ITERS)
        def _():
            for o in range(orbs):
                out_dressed[o] = values[o]

    def couplings(turn):
        def one(i):
            halves = [
                dot(inter[i, k], amps_now[couple[i, k] % pairs]).astype(bf16)
                for k in range(partners)
            ]
            coupled[i] = dot(jnp.concatenate(halves, axis=1), inter_t[i])

        for i in range(own_pairs):
            one(i)

    def finish(turn):
        for first in range(0, own_pairs, BATCH):
            batch = range(first, min(first + BATCH, own_pairs))
            for i in batch:
                part_wait(turn, i)
            totals = {}
            for i in batch:
                total = parts_out[turn, i, 0].astype(jnp.float32)
                for step in range(1, 3 if square else ranks):
                    total += parts_in[turn, i, step - 1].astype(jnp.float32)
                totals[i] = total.astype(bf16)
            rights = {i: dot(totals[i], maps[own + i, 1]).astype(bf16) for i in batch}
            values = {
                i: (dot(first_t[own + i], rights[i]) + coupled[i]) * scale[i] for i in batch
            }

            @pl.when(turn + 1 < ITERS)
            def _(batch=batch, values=values):
                for i in batch:
                    amps[turn + 1, own + i] = values[i].astype(bf16)
                    amp_start(turn + 1, i)

            @pl.when(turn + 1 == ITERS)
            def _(batch=batch, values=values):
                for i in batch:
                    out_amps[i] = values[i]

    win_start(0, True)
    orb_copy = pltpu.make_async_copy(orb_hbm, window.at[0, middle], orb_sem)
    orb_copy.start()
    small_copies[0].wait()
    for i in range(own_pairs):
        amps[0, own + i] = amplitudes[i].astype(bf16)
    for i in range(own_pairs):
        amp_start(0, i)
    for copy in small_copies[1:]:
        copy.start()
    maps_copy = pltpu.make_async_copy(maps_hbm, maps, maps_sem)
    maps_copy.start()
    inter_copy = pltpu.make_async_copy(inter_hbm, inter, inter_sem)
    inter_copy.start()

    for copy in small_copies[1:]:
        copy.wait()

    @pl.loop(0, pairs)
    def _(pair):
        second = occ_second[pair]
        distance = (second // orbs - group + REACH + groups) % groups
        second_at[pair] = jnp.minimum(distance, SIDES - 1) * orbs + second % orbs

    orb_copy.wait()
    transposed(0)
    maps_copy.wait()

    @pl.loop(0, ranks)
    def _(block):
        for i in range(own_pairs):
            first_t[block * own_pairs + i] = maps[block * own_pairs + i, 0].T

    inter_copy.wait()

    @pl.loop(0, own_pairs)
    def _(i):
        rows = jnp.broadcast_to(pno_energy[pl.ds(i, 1), :], (size, size))
        denominator = rows + rows.T
        denominator -= occ_energy[occ_first[own + i]]
        denominator -= occ_energy[occ_second[own + i]]
        scale[i] = -1.0 / denominator
        for k in range(partners):
            inter_t[i, k * size : (k + 1) * size, :] = inter[i, k].T

    near_steps = (0, 1, 2) if square else (0,)
    far_steps = (3,) if square else tuple(range(1, ranks))

    def throughs(turn, some):
        if square:
            for step in some:
                if step > 0:
                    amp_wait(turn, step)
        first, last = some[0], some[-1] + 1

        @pl.loop(first, last)
        def _(step):
            if not square and first > 0:
                amp_wait(turn, step)
            through(turn, step)

    near_steps = (0, 1, 2) if square else (0,)
    far_steps = (3,) if square else tuple(range(1, ranks))
    inner = group % 2 == 1

    throughs(0, (0,))
    if square:
        relay_all(0)

    @pl.loop(0, ITERS)
    def _(turn):
        integrals(turn)

        if square:

            @pl.when(turn == 0)
            def _():
                far_sums(turn)

            @pl.when(turn > 0)
            def _():
                @pl.when(jnp.logical_not(inner))
                def _():
                    far_sums(turn)

                throughs(turn, (0,))
                relay_all(turn)

                @pl.when(jnp.logical_not(inner))
                def _():
                    near_sums(turn)

            throughs(turn, (1, 2))
        else:

            @pl.when(turn > 0)
            def _():
                throughs(turn, (0,))

        fit_near(turn)
        if square:

            @pl.when(turn > 0)
            def _():
                @pl.when(inner)
                def _():
                    far_sums(turn)
                    near_sums(turn)

                forward_all(turn)

        throughs(turn, far_steps)
        dress(turn)

        @pl.when(turn + 1 < ITERS)
        def _():
            win_start(turn + 1)
            if square:
                near_sums(turn)
                forward_all(turn)
            transposed(turn + 1)

        couplings(turn)

        @pl.when(turn > 0)
        def _():
            sent(turn - 1)
            parts_sent(turn - 1)

        finish(turn)

    sent(ITERS - 1)
    parts_sent(ITERS - 1)


def store(amps, dressed, out_amps, out_dressed, sem):
    copies = [
        pltpu.make_async_copy(amps, out_amps, sem.at[0]),
        pltpu.make_async_copy(dressed, out_dressed, sem.at[1]),
    ]
    for copy in copies:
        copy.start()
    for copy in copies:
        copy.wait()


def on_device(
    ranks,
    groups,
    amplitudes,
    couple,
    occ_first,
    occ_second,
    couple_intersection,
    pno_maps,
    orbital_blocks,
    pno_energy,
    occ_energy,
):
    own_pairs, size, _ = amplitudes.shape
    group_pairs = occ_first.shape[0]
    orbs, rows, virtuals = orbital_blocks.shape
    partners = couple.shape[1]
    bf16 = jnp.bfloat16
    vmem = pl.BlockSpec(memory_space=pltpu.VMEM)
    hbm = pl.BlockSpec(memory_space=pltpu.HBM)
    dma = pltpu.SemaphoreType.DMA
    results = pl.pallas_call(
        functools.partial(kernel, ranks, groups),
        out_shape=(
            pltpu.VMEM(amplitudes.shape, jnp.float32),
            pltpu.VMEM(orbital_blocks.shape, jnp.float32),
        ),
        in_specs=[hbm] * 9,
        out_specs=(vmem, vmem),
        scratch_shapes=[
            pltpu.SMEM(couple.shape, couple.dtype),
            pltpu.SMEM(occ_first.shape, occ_first.dtype),
            pltpu.SMEM(occ_second.shape, occ_second.dtype),
            pltpu.SMEM(occ_energy.shape, occ_energy.dtype),
            pltpu.SMEM(occ_second.shape, occ_second.dtype),
            pltpu.VMEM(amplitudes.shape, amplitudes.dtype),
            pltpu.VMEM(pno_energy.shape, pno_energy.dtype),
            pltpu.VMEM(couple_intersection.shape, bf16),
            pltpu.VMEM((own_pairs, partners * size, size), bf16),
            pltpu.VMEM(pno_maps.shape, bf16),
            pltpu.VMEM((group_pairs, size, virtuals), bf16),
            pltpu.VMEM((orbs, virtuals, rows), bf16),
            pltpu.VMEM((own_pairs, size, size), jnp.float32),
            pltpu.VMEM((own_pairs, size, size), jnp.float32),
            pltpu.VMEM((ITERS, group_pairs, size, size), bf16),
            pltpu.VMEM((group_pairs, size, size), bf16),
            pltpu.VMEM((ITERS, SIDES * orbs, rows, virtuals), bf16),
            pltpu.VMEM((SIDES * orbs, rows, virtuals), bf16),
            pltpu.VMEM((ITERS, own_pairs, ranks, virtuals, virtuals), bf16),
            pltpu.VMEM((ITERS, own_pairs, ranks - 1, virtuals, virtuals), bf16),
            pltpu.VMEM((ITERS, own_pairs, virtuals, virtuals), bf16),
            pltpu.VMEM((group_pairs * virtuals, orbs * virtuals), bf16),
            pltpu.VMEM((rows, orbs * virtuals), jnp.float32),
            dma((ITERS,)),
            dma((ITERS, ranks, own_pairs)),
            dma((ITERS,)),
            dma((ITERS, SIDES)),
            dma((ITERS,)),
            dma((ITERS, own_pairs)),
            dma((ITERS, own_pairs)),
            dma,
            dma,
            dma,
            dma((6,)),
        ],
        compiler_params=pltpu.CompilerParams(
            collective_id=0, has_side_effects=True, vmem_limit_bytes=67043328 - 4096 * 1024
        ),
    )(
        *(pltpu.with_memory_space_constraint(x, pltpu.HBM) for x in (
        couple,
        occ_first,
        occ_second,
        occ_energy,
        amplitudes,
        pno_energy,
        couple_intersection,
        pno_maps,
        orbital_blocks,
        ))
    )
    return pl.pallas_call(
        store,
        out_shape=tuple(pltpu.HBM(x.shape, x.dtype) for x in results),
        in_specs=[vmem] * 2,
        out_specs=(hbm, hbm),
        scratch_shapes=[dma((2,))],
        compiler_params=pltpu.CompilerParams(vmem_limit_bytes=4096 * 1024),
    )(*(pltpu.with_memory_space_constraint(x, pltpu.VMEM) for x in results))


def solution(mesh):
    return jax.shard_map(
        functools.partial(on_device, mesh.shape["orb"], mesh.shape["pair"]),
        mesh=mesh,
        in_specs=(
            P(("pair", "orb"), None, None),
            P(("pair", "orb"), None),
            P("pair"),
            P("pair"),
            P(("pair", "orb"), None, None, None),
            P("pair", None, None, None),
            P("pair", "orb", None),
            P(("pair", "orb"), None),
            P(),
        ),
        out_specs=(P(("pair", "orb"), None, None), P("pair", "orb", None)),
        check_vma=False,
    )
```

time: 30.9 us -> 30.3 us (0.981)
  Pallas kernels: 30.1 us -> 29.5 us
    pallas_call x1, Pallas kernels: 29.3 us -> 28.7 us  [on_device(): pl.pallas_call(functools.partial(kernel, ranks, groups), out_shape=(pltpu...]
where the time goes in v2:
time: 30.3 us; the launch traced here: 30.1 us
  Pallas kernels  29.5 us (97%)
  between operations  0.64 us (2%)
    pallas_call x1, Pallas kernels, on_device(): pl.pallas_call(functools.partial(kernel, ranks, groups), out_shape=(pltpu...  28.7 us
    pallas_call x1, Pallas kernels, on_device(): pl.pallas_call(store, out_shape=tuple((pltpu.HBM(x.shape, x.dtype) for x...  0.81 us

profile of v2, /device:TPU:0, one launch (start us, length us, event | category | flops | bytes accessed | tf_op | source)
XLA Modules:
  0.0 30.1 jit_solution(4741880685624894729)
XLA Ops:
  0.6 28.7 %shard_map.104 = (f32[4,128,128]{2,1,0:T(8,128)S(1)}, f32[4,128,128]{2,1,0:T(8,128)S(1)}) custom-call(s32[4,16]{1,0:T(4,128)} %couple_hbm.1, s32[16]{0:T(128)} %first_hbm.1, s32[16]{0:T(128)} %second_hbm.1, f32[32]{0:T(128)} %energy_hbm.1, f32[4,128,128]{2,1,0:T(8,128)} %amps_hbm.1, f32[4,128]{1,0:T(4,128)} %pno_hbm.1, bf16[4,16,128,128]{3,2,1,0:T(8,128)(2,1)} %inter_hbm.1, ...), custom_call_target="tpu_custom_call" | custom-call | tf_op jit(solution)/shard_map/pallas_call | solution.py:536
  29.3 0.8 %shard_map.105 = (f32[4,128,128]{2,1,0:T(8,128)}, f32[4,128,128]{2,1,0:T(8,128)}) custom-call(f32[4,128,128]{2,1,0:T(8,128)S(1)} %get-tuple-element.4.amps, f32[4,128,128]{2,1,0:T(8,128)S(1)} %get-tuple-element.5.dressed), custom_call_target="tpu_custom_call" | custom-call | tf_op jit(solution)/shard_map/pallas_call | solution.py:596

commit v3 on v2

--- a/solution.py
+++ b/solution.py
@@ -13,6 +13,12 @@
 
 dress_scale = 0.015
 BATCH = 2
+GATHER_DIRECT = ("none", "none")
+SUM_DIRECT = ("outer", "none")
+NONE = ("none", "none")
+FIRST_RELAY = "all"
+INNER_FAR = 1
+INNER_NEAR = 2
 
 NN = (((1,), (0,)), ((), ()))
 NT = (((1,), (1,)), ((), ()))
@@ -95,6 +101,29 @@
     def source(step):
         return target(step) if square else (me + ranks - step) % ranks
 
+    inner = group % 2 == 1
+
+    def kinds(modes, turn):
+        flags = [{"none": False, "all": True, "outer": jnp.logical_not(inner)}[m] for m in modes]
+        if isinstance(turn, int):
+            return flags[turn]
+        if all(mode == modes[0] for mode in modes):
+            return flags[0]
+        flag = False
+        for at in range(ITERS):
+            flag = jnp.logical_or(flag, jnp.logical_and(turn == at, flags[at]))
+        return flag
+
+    def either(flag, yes, no):
+        if isinstance(flag, bool):
+            (yes if flag else no)()
+        else:
+            pl.when(flag)(yes)
+            pl.when(jnp.logical_not(flag))(no)
+
+    def nothing():
+        pass
+
     barrier = pltpu.get_barrier_semaphore()
     for step in range(1, ranks):
         pl.semaphore_signal(
@@ -163,7 +192,7 @@
     def relay_all(turn):
         for i in range(own_pairs):
             amp_copy(turn, 1 if i % 2 == 0 else 2, i).wait_recv()
-            amp_relay(turn, i).start()
+            either(kinds(GATHER_DIRECT, turn), nothing, amp_relay(turn, i).start)
 
     def amp_wait(turn, step):
         for i in range(own_pairs):
@@ -194,13 +223,16 @@
         )
 
     def forward_all(turn):
-        for i in range(own_pairs):
-            onto = 2 if i % 2 == 0 else 1
-            part_relay(turn, i).wait_recv()
-            total = parts_out[turn, i, onto].astype(jnp.float32)
-            total += relayed[turn, i].astype(jnp.float32)
-            parts_out[turn, i, onto] = total.astype(bf16)
-            part_copy(turn, onto, i).start()
+        def relays():
+            for i in range(own_pairs):
+                onto = 2 if i % 2 == 0 else 1
+                part_relay(turn, i).wait_recv()
+                total = parts_out[turn, i, onto].astype(jnp.float32)
+                total += relayed[turn, i].astype(jnp.float32)
+                parts_out[turn, i, onto] = total.astype(bf16)
+                part_copy(turn, onto, i).start()
+
+        either(kinds(SUM_DIRECT, turn), nothing, relays)
 
     def whole(ref, send_sem, recv_sem):
         return pltpu.make_async_remote_copy(
@@ -217,7 +249,10 @@
             arrived = parts_in.at[turn, i, pl.ds(0, terms)]
             whole(arrived, part_send.at[turn], part_recv.at[turn, i]).wait_recv()
 
-        wait(2 if square else ranks - 1)
+        if square:
+            either(kinds(SUM_DIRECT, turn), lambda: wait(3), lambda: wait(2))
+        else:
+            wait(ranks - 1)
 
     def sent(turn):
         sends = pl.ds(0, (ranks - 1) * own_pairs)
@@ -229,6 +264,8 @@
         whole(parts_in.at[turn], part_send.at[turn], part_recv.at[turn, 0]).wait_send()
 
     def amp_start(turn, i):
+        if square:
+            either(kinds(GATHER_DIRECT, turn), amp_copy(turn, 3, i).start, nothing)
         for step in (1, 2) if square else range(ranks - 1, 0, -1):
             amp_copy(turn, step, i).start()
 
@@ -267,12 +304,23 @@
             pl.loop(0, own_pairs)(one)
 
     def far_sums(turn):
-        for i in range(own_pairs):
-            part_relay(turn, i).start()
+        def direct():
+            for i in range(own_pairs):
+                for step in (3, 1, 2):
+                    part_copy(turn, step, i).start()
+
+        def relays():
+            for i in range(own_pairs):
+                part_relay(turn, i).start()
+
+        either(kinds(SUM_DIRECT, turn), direct, relays)
 
     def near_sums(turn):
-        for i in range(own_pairs):
-            part_copy(turn, 1 if i % 2 == 0 else 2, i).start()
+        def relays():
+            for i in range(own_pairs):
+                part_copy(turn, 1 if i % 2 == 0 else 2, i).start()
+
+        either(kinds(SUM_DIRECT, turn), nothing, relays)
 
     def through(turn, step):
         base = source(step) * own_pairs
@@ -347,7 +395,7 @@
             totals = {}
             for i in batch:
                 total = parts_out[turn, i, 0].astype(jnp.float32)
-                for step in range(1, 3 if square else ranks):
+                for step in range(1, ranks if SUM_DIRECT != NONE or not square else 3):
                     total += parts_in[turn, i, step - 1].astype(jnp.float32)
                 totals[i] = total.astype(bf16)
             rights = {i: dot(totals[i], maps[own + i, 1]).astype(bf16) for i in batch}
@@ -390,6 +438,15 @@
         distance = (second // orbs - group + REACH + groups) % groups
         second_at[pair] = jnp.minimum(distance, SIDES - 1) * orbs + second % orbs
 
+    if square and SUM_DIRECT != NONE:
+        for turn in range(ITERS):
+
+            def zero(turn=turn):
+                for i in range(own_pairs):
+                    parts_in[turn, i, 2] = jnp.zeros_like(parts_in[turn, i, 2])
+
+            either(kinds(SUM_DIRECT, turn), nothing, zero)
+
     orb_copy.wait()
     transposed(0)
     maps_copy.wait()
@@ -429,11 +486,19 @@
 
     near_steps = (0, 1, 2) if square else (0,)
     far_steps = (3,) if square else tuple(range(1, ranks))
-    inner = group % 2 == 1
-
     throughs(0, (0,))
+    relay_first = {"all": True, "inner": inner, "none": False}[FIRST_RELAY]
     if square:
-        relay_all(0)
+        either(relay_first, lambda: relay_all(0), nothing)
+
+    def sums(turn, place):
+        def some(far_place, near_place):
+            if far_place == place:
+                far_sums(turn)
+            if near_place == place:
+                near_sums(turn)
+
+        either(inner, lambda: some(INNER_FAR, INNER_NEAR), lambda: some(0, 1))
 
     @pl.loop(0, ITERS)
     def _(turn):
@@ -444,19 +509,14 @@
             @pl.when(turn == 0)
             def _():
                 far_sums(turn)
+                either(relay_first, nothing, lambda: relay_all(0))
 
             @pl.when(turn > 0)
             def _():
-                @pl.when(jnp.logical_not(inner))
-                def _():
-                    far_sums(turn)
-
+                sums(turn, 0)
                 throughs(turn, (0,))
                 relay_all(turn)
-
-                @pl.when(jnp.logical_not(inner))
-                def _():
-                    near_sums(turn)
+                sums(turn, 1)
 
             throughs(turn, (1, 2))
         else:
@@ -470,11 +530,7 @@
 
             @pl.when(turn > 0)
             def _():
-                @pl.when(inner)
-                def _():
-                    far_sums(turn)
-                    near_sums(turn)
-
+                sums(turn, 2)
                 forward_all(turn)
 
         throughs(turn, far_steps)

time: 30.3 us -> 29.1 us (0.960)
  Pallas kernels: 29.5 us -> 28.3 us
    pallas_call x1, Pallas kernels: 28.7 us -> 27.5 us  [on_device(): pl.pallas_call(functools.partial(kernel, ranks, groups), out_shape=(pltpu...]
where the time goes in v3:
time: 29.1 us; the launch traced here: 28.9 us
  Pallas kernels  28.3 us (97%)
  between operations  0.64 us (2%)
    pallas_call x1, Pallas kernels, on_device(): pl.pallas_call(functools.partial(kernel, ranks, groups), out_shape=(pltpu...  27.5 us
    pallas_call x1, Pallas kernels, on_device(): pl.pallas_call(store, out_shape=tuple((pltpu.HBM(x.shape, x.dtype) for x...  0.81 us

profile of v3, /device:TPU:0, one launch (start us, length us, event | category | flops | bytes accessed | tf_op | source)
XLA Modules:
  0.0 28.9 jit_solution(18281175789316911558)
XLA Ops:
  0.6 27.5 %shard_map.104 = (f32[4,128,128]{2,1,0:T(8,128)S(1)}, f32[4,128,128]{2,1,0:T(8,128)S(1)}) custom-call(s32[4,16]{1,0:T(4,128)} %couple_hbm.1, s32[16]{0:T(128)} %first_hbm.1, s32[16]{0:T(128)} %second_hbm.1, f32[32]{0:T(128)} %energy_hbm.1, f32[4,128,128]{2,1,0:T(8,128)} %amps_hbm.1, f32[4,128]{1,0:T(4,128)} %pno_hbm.1, bf16[4,16,128,128]{3,2,1,0:T(8,128)(2,1)} %inter_hbm.1, ...), custom_call_target="tpu_custom_call" | custom-call | tf_op jit(solution)/shard_map/pallas_call | solution.py:592
  28.1 0.8 %shard_map.105 = (f32[4,128,128]{2,1,0:T(8,128)}, f32[4,128,128]{2,1,0:T(8,128)}) custom-call(f32[4,128,128]{2,1,0:T(8,128)S(1)} %get-tuple-element.4.amps, f32[4,128,128]{2,1,0:T(8,128)S(1)} %get-tuple-element.5.dressed), custom_call_target="tpu_custom_call" | custom-call | tf_op jit(solution)/shard_map/pallas_call | solution.py:652

commit v4 on v3

--- a/solution.py
+++ b/solution.py
@@ -13,10 +13,11 @@
 
 dress_scale = 0.015
 BATCH = 2
-GATHER_DIRECT = ("none", "none")
 SUM_DIRECT = ("outer", "none")
 NONE = ("none", "none")
 FIRST_RELAY = "all"
+EARLY_NEAR = True
+NEAR_AT = 0
 INNER_FAR = 1
 INNER_NEAR = 2
 
@@ -89,7 +90,7 @@
     middle = pl.ds(REACH * orbs, orbs)
     places = [place for place in range(SIDES) if place != REACH]
     bf16 = jnp.bfloat16
-    square = ranks == 4 and own_pairs % 2 == 0
+    square = ranks == 4 and own_pairs % BATCH == 0
     z_place = (group + 1) % 2 * 2 * REACH
     c_place = 2 * REACH - z_place
 
@@ -162,17 +163,25 @@
             src_ref=orb_hbm if bare else window.at[turn, middle],
             dst_ref=window.at[turn, pl.ds(place * orbs, orbs)],
             send_sem=win_send.at[turn],
-            recv_sem=win_recv.at[turn, place],
+            recv_sem=win_recv.at[turn],
             device_id={"pair": (group + REACH - place + groups) % groups},
             device_id_type=pl.DeviceIdType.MESH,
         )
+
+    def relayed_tile(step, i):
+        return (step, i % 2) in ((1, 0), (2, 1))
+
+    def amp_slot(step, i):
+        if not square:
+            return step
+        return i if relayed_tile(step, i) else own_pairs
 
     def amp_copy(turn, step, i):
         return pltpu.make_async_remote_copy(
             src_ref=amps.at[turn, own + i],
             dst_ref=amps.at[turn, own + i],
             send_sem=amp_send.at[turn],
-            recv_sem=amp_recv.at[turn, step, i],
+            recv_sem=amp_recv.at[turn, amp_slot(step, i)],
             device_id={"orb": target(step)},
             device_id_type=pl.DeviceIdType.MESH,
         )
@@ -184,7 +193,7 @@
             src_ref=amps.at[turn, place],
             dst_ref=amps.at[turn, place],
             send_sem=amp_send.at[turn],
-            recv_sem=amp_recv.at[turn, 3, i],
+            recv_sem=amp_recv.at[turn, own_pairs + 1],
             device_id={"orb": target(onto)},
             device_id_type=pl.DeviceIdType.MESH,
         )
@@ -192,22 +201,18 @@
     def relay_all(turn):
         for i in range(own_pairs):
             amp_copy(turn, 1 if i % 2 == 0 else 2, i).wait_recv()
-            either(kinds(GATHER_DIRECT, turn), nothing, amp_relay(turn, i).start)
-
-    def amp_wait(turn, step):
-        for i in range(own_pairs):
-            def wait(i=i):
-                amp_copy(turn, step, i).wait_recv()
-
-            if not square or step == 3 or (step, i % 2) in ((1, 1), (2, 0)):
-                wait()
+            amp_relay(turn, i).start()
+
+    def amp_wait(turn, slot):
+        block = amps.at[turn, pl.ds(own, own_pairs)]
+        whole(block, amp_send.at[turn], amp_recv.at[turn, slot]).wait_recv()
 
     def part_copy(turn, step, i):
         return pltpu.make_async_remote_copy(
             src_ref=parts_out.at[turn, i, step],
-            dst_ref=parts_in.at[turn, i, step - 1],
+            dst_ref=parts_in.at[turn, i // BATCH, step - 1, i % BATCH],
             send_sem=part_send.at[turn],
-            recv_sem=part_recv.at[turn, i],
+            recv_sem=part_recv.at[turn, i // BATCH],
             device_id={"orb": target(step)},
             device_id_type=pl.DeviceIdType.MESH,
         )
@@ -217,20 +222,23 @@
             src_ref=parts_out.at[turn, i, 3],
             dst_ref=relayed.at[turn, i],
             send_sem=part_send.at[turn],
-            recv_sem=relay_recv.at[turn, i],
+            recv_sem=relay_recv.at[turn, i // BATCH],
             device_id={"orb": target(1 if i % 2 == 0 else 2)},
             device_id_type=pl.DeviceIdType.MESH,
         )
 
     def forward_all(turn):
         def relays():
-            for i in range(own_pairs):
-                onto = 2 if i % 2 == 0 else 1
-                part_relay(turn, i).wait_recv()
-                total = parts_out[turn, i, onto].astype(jnp.float32)
-                total += relayed[turn, i].astype(jnp.float32)
-                parts_out[turn, i, onto] = total.astype(bf16)
-                part_copy(turn, onto, i).start()
+            for first in range(0, own_pairs, BATCH):
+                arrived = relayed.at[turn, pl.ds(first, BATCH)]
+                whole(arrived, part_send.at[turn], relay_recv.at[turn, first // BATCH]).wait_recv()
+                for i in range(first, first + BATCH):
+                    onto = 2 if i % 2 == 0 else 1
+                    total = parts_out[turn, i, onto].astype(jnp.float32)
+                    total += relayed[turn, i].astype(jnp.float32)
+                    parts_out[turn, i, onto] = total.astype(bf16)
+                for i in range(first, first + BATCH):
+                    part_copy(turn, 2 if i % 2 == 0 else 1, i).start()
 
         either(kinds(SUM_DIRECT, turn), nothing, relays)
 
@@ -244,10 +252,10 @@
             device_id_type=pl.DeviceIdType.MESH,
         )
 
-    def part_wait(turn, i):
+    def part_wait(turn, at):
         def wait(terms):
-            arrived = parts_in.at[turn, i, pl.ds(0, terms)]
-            whole(arrived, part_send.at[turn], part_recv.at[turn, i]).wait_recv()
+            arrived = parts_in.at[turn, at, pl.ds(0, terms)]
+            whole(arrived, part_send.at[turn], part_recv.at[turn, at]).wait_recv()
 
         if square:
             either(kinds(SUM_DIRECT, turn), lambda: wait(3), lambda: wait(2))
@@ -256,18 +264,25 @@
 
     def sent(turn):
         sends = pl.ds(0, (ranks - 1) * own_pairs)
-        whole(amps.at[turn, sends], amp_send.at[turn], amp_recv.at[turn, 0, 0]).wait_send()
+        whole(amps.at[turn, sends], amp_send.at[turn], amp_recv.at[turn, 0]).wait_send()
         sends = pl.ds(0, len(places) * orbs)
-        whole(window.at[turn, sends], win_send.at[turn], win_recv.at[turn, 0]).wait_send()
+        whole(window.at[turn, sends], win_send.at[turn], win_recv.at[turn]).wait_send()
 
     def parts_sent(turn):
         whole(parts_in.at[turn], part_send.at[turn], part_recv.at[turn, 0]).wait_send()
 
     def amp_start(turn, i):
+        for step in range(ranks - 1, 0, -1):
+            amp_copy(turn, step, i).start()
+
+    def amps_start(turn, batch):
         if square:
-            either(kinds(GATHER_DIRECT, turn), amp_copy(turn, 3, i).start, nothing)
-        for step in (1, 2) if square else range(ranks - 1, 0, -1):
-            amp_copy(turn, step, i).start()
+            for turned in (0, 1):
+                for i in batch:
+                    amp_copy(turn, 1 if (i + turned) % 2 == 0 else 2, i).start()
+        else:
+            for i in batch:
+                amp_start(turn, i)
 
     def win_start(turn, bare=False):
         win_copy(turn, z_place, bare).start()
@@ -283,8 +298,8 @@
         parts_out[turn, i, step] = dot(left, blocks[second_at[pair]]).astype(bf16)
 
     def integrals(turn):
-        for place in places:
-            win_copy(turn, place).wait_recv()
+        arrivals = window.at[turn, pl.ds(0, len(places) * orbs)]
+        whole(arrivals, win_send.at[turn], win_recv.at[turn]).wait_recv()
         for at in range(SIDES * orbs):
             blocks[at] = window[turn, at]
 
@@ -390,13 +405,12 @@
     def finish(turn):
         for first in range(0, own_pairs, BATCH):
             batch = range(first, min(first + BATCH, own_pairs))
-            for i in batch:
-                part_wait(turn, i)
+            part_wait(turn, first // BATCH)
             totals = {}
             for i in batch:
                 total = parts_out[turn, i, 0].astype(jnp.float32)
                 for step in range(1, ranks if SUM_DIRECT != NONE or not square else 3):
-                    total += parts_in[turn, i, step - 1].astype(jnp.float32)
+                    total += parts_in[turn, i // BATCH, step - 1, i % BATCH].astype(jnp.float32)
                 totals[i] = total.astype(bf16)
             rights = {i: dot(totals[i], maps[own + i, 1]).astype(bf16) for i in batch}
             values = {
@@ -407,7 +421,7 @@
             def _(batch=batch, values=values):
                 for i in batch:
                     amps[turn + 1, own + i] = values[i].astype(bf16)
-                    amp_start(turn + 1, i)
+                amps_start(turn + 1, batch)
 
             @pl.when(turn + 1 == ITERS)
             def _(batch=batch, values=values):
@@ -420,8 +434,7 @@
     small_copies[0].wait()
     for i in range(own_pairs):
         amps[0, own + i] = amplitudes[i].astype(bf16)
-    for i in range(own_pairs):
-        amp_start(0, i)
+    amps_start(0, range(own_pairs))
     for copy in small_copies[1:]:
         copy.start()
     maps_copy = pltpu.make_async_copy(maps_hbm, maps, maps_sem)
@@ -443,7 +456,7 @@
 
             def zero(turn=turn):
                 for i in range(own_pairs):
-                    parts_in[turn, i, 2] = jnp.zeros_like(parts_in[turn, i, 2])
+                    parts_in[turn, i // BATCH, 2, i % BATCH] = jnp.zeros((size, size), bf16)
 
             either(kinds(SUM_DIRECT, turn), nothing, zero)
 
@@ -472,11 +485,9 @@
     far_steps = (3,) if square else tuple(range(1, ranks))
 
     def throughs(turn, some):
-        if square:
-            for step in some:
-                if step > 0:
-                    amp_wait(turn, step)
         first, last = some[0], some[-1] + 1
+        if square and first > 0:
+            amp_wait(turn, own_pairs + (0 if first == 1 else 1))
 
         @pl.loop(first, last)
         def _(step):
@@ -490,6 +501,8 @@
     relay_first = {"all": True, "inner": inner, "none": False}[FIRST_RELAY]
     if square:
         either(relay_first, lambda: relay_all(0), nothing)
+        if EARLY_NEAR:
+            either(inner, lambda: throughs(0, (1, 2)), nothing)
 
     def sums(turn, place):
         def some(far_place, near_place):
@@ -509,7 +522,8 @@
             @pl.when(turn == 0)
             def _():
                 far_sums(turn)
-                either(relay_first, nothing, lambda: relay_all(0))
+                if NEAR_AT == 0:
+                    near_sums(turn)
 
             @pl.when(turn > 0)
             def _():
@@ -518,7 +532,14 @@
                 relay_all(turn)
                 sums(turn, 1)
 
-            throughs(turn, (1, 2))
+            if EARLY_NEAR:
+
+                @pl.when(jnp.logical_or(turn > 0, jnp.logical_not(inner)))
+                def _():
+                    throughs(turn, (1, 2))
+
+            else:
+                throughs(turn, (1, 2))
         else:
 
             @pl.when(turn > 0)
@@ -540,8 +561,11 @@
         def _():
             win_start(turn + 1)
             if square:
-                near_sums(turn)
+                if NEAR_AT == 1:
+                    near_sums(turn)
                 forward_all(turn)
+                if NEAR_AT == 2:
+                    near_sums(turn)
             transposed(turn + 1)
 
         couplings(turn)
@@ -589,6 +613,7 @@
     vmem = pl.BlockSpec(memory_space=pltpu.VMEM)
     hbm = pl.BlockSpec(memory_space=pltpu.HBM)
     dma = pltpu.SemaphoreType.DMA
+    square = ranks == 4 and own_pairs % BATCH == 0
     results = pl.pallas_call(
         functools.partial(kernel, ranks, groups),
         out_shape=(
@@ -617,17 +642,17 @@
             pltpu.VMEM((ITERS, SIDES * orbs, rows, virtuals), bf16),
             pltpu.VMEM((SIDES * orbs, rows, virtuals), bf16),
             pltpu.VMEM((ITERS, own_pairs, ranks, virtuals, virtuals), bf16),
-            pltpu.VMEM((ITERS, own_pairs, ranks - 1, virtuals, virtuals), bf16),
+            pltpu.VMEM((ITERS, own_pairs // BATCH, ranks - 1, BATCH, virtuals, virtuals), bf16),
             pltpu.VMEM((ITERS, own_pairs, virtuals, virtuals), bf16),
             pltpu.VMEM((group_pairs * virtuals, orbs * virtuals), bf16),
             pltpu.VMEM((rows, orbs * virtuals), jnp.float32),
             dma((ITERS,)),
-            dma((ITERS, ranks, own_pairs)),
+            dma((ITERS, own_pairs + 2 if square else ranks)),
             dma((ITERS,)),
-            dma((ITERS, SIDES)),
             dma((ITERS,)),
-            dma((ITERS, own_pairs)),
-            dma((ITERS, own_pairs)),
+            dma((ITERS,)),
+            dma((ITERS, own_pairs // BATCH)),
+            dma((ITERS, own_pairs // BATCH)),
             dma,
             dma,
             dma,

time: 29.1 us -> 28.4 us (0.976)
  Pallas kernels: 28.3 us -> 27.6 us
    pallas_call x1, Pallas kernels: 27.5 us -> 26.8 us  [on_device(): pl.pallas_call(functools.partial(kernel, ranks, groups), out_shape=(pltpu...]
where the time goes in v4:
time: 28.4 us; the launch traced here: 28.2 us
  Pallas kernels  27.6 us (97%)
  between operations  0.64 us (2%)
    pallas_call x1, Pallas kernels, on_device(): pl.pallas_call(functools.partial(kernel, ranks, groups), out_shape=(pltpu...  26.8 us
    pallas_call x1, Pallas kernels, on_device(): pl.pallas_call(store, out_shape=tuple((pltpu.HBM(x.shape, x.dtype) for x...  0.81 us

profile of v4, /device:TPU:0, one launch (start us, length us, event | category | flops | bytes accessed | tf_op | source)
XLA Modules:
  0.0 28.2 jit_solution(7537302726288815285)
XLA Ops:
  0.6 26.8 %shard_map.104 = (f32[4,128,128]{2,1,0:T(8,128)S(1)}, f32[4,128,128]{2,1,0:T(8,128)S(1)}) custom-call(s32[4,16]{1,0:T(4,128)} %couple_hbm.1, s32[16]{0:T(128)} %first_hbm.1, s32[16]{0:T(128)} %second_hbm.1, f32[32]{0:T(128)} %energy_hbm.1, f32[4,128,128]{2,1,0:T(8,128)} %amps_hbm.1, f32[4,128]{1,0:T(4,128)} %pno_hbm.1, bf16[4,16,128,128]{3,2,1,0:T(8,128)(2,1)} %inter_hbm.1, ...), custom_call_target="tpu_custom_call" | custom-call | tf_op jit(solution)/shard_map/pallas_call | solution.py:617
  27.4 0.8 %shard_map.105 = (f32[4,128,128]{2,1,0:T(8,128)}, f32[4,128,128]{2,1,0:T(8,128)}) custom-call(f32[4,128,128]{2,1,0:T(8,128)S(1)} %get-tuple-element.4.amps, f32[4,128,128]{2,1,0:T(8,128)S(1)} %get-tuple-element.5.dressed), custom_call_target="tpu_custom_call" | custom-call | tf_op jit(solution)/shard_map/pallas_call | solution.py:677

commit v5 on v4

--- a/solution.py
+++ b/solution.py
@@ -285,8 +285,8 @@
                 amp_start(turn, i)
 
     def win_start(turn, bare=False):
+        win_copy(turn, c_place, bare).start()
         win_copy(turn, z_place, bare).start()
-        win_copy(turn, c_place, bare).start()
 
     def transposed(turn):
         for o in range(orbs):
@@ -552,7 +552,7 @@
             @pl.when(turn > 0)
             def _():
                 sums(turn, 2)
-                forward_all(turn)
+                either(inner, nothing, lambda: forward_all(turn))
 
         throughs(turn, far_steps)
         dress(turn)
@@ -567,6 +567,12 @@
                 if NEAR_AT == 2:
                     near_sums(turn)
             transposed(turn + 1)
+
+        if square:
+
+            @pl.when(jnp.logical_and(turn > 0, inner))
+            def _():
+                forward_all(turn)
 
         couplings(turn)
 

time: 28.4 us -> 28.4 us (level)
  no operation moved by 1% of the time
where the time goes in v5:
time: 28.4 us; the launch traced here: 28.2 us
  Pallas kernels  27.6 us (97%)
  between operations  0.64 us (2%)
    pallas_call x1, Pallas kernels, on_device(): pl.pallas_call(functools.partial(kernel, ranks, groups), out_shape=(pltpu...  26.8 us
    pallas_call x1, Pallas kernels, on_device(): pl.pallas_call(store, out_shape=tuple((pltpu.HBM(x.shape, x.dtype) for x...  0.81 us

profile of v5, /device:TPU:0, one launch (start us, length us, event | category | flops | bytes accessed | tf_op | source)
XLA Modules:
  0.0 28.2 jit_solution(1473955935848074504)
XLA Ops:
  0.6 26.8 %shard_map.104 = (f32[4,128,128]{2,1,0:T(8,128)S(1)}, f32[4,128,128]{2,1,0:T(8,128)S(1)}) custom-call(s32[4,16]{1,0:T(4,128)} %couple_hbm.1, s32[16]{0:T(128)} %first_hbm.1, s32[16]{0:T(128)} %second_hbm.1, f32[32]{0:T(128)} %energy_hbm.1, f32[4,128,128]{2,1,0:T(8,128)} %amps_hbm.1, f32[4,128]{1,0:T(4,128)} %pno_hbm.1, bf16[4,16,128,128]{3,2,1,0:T(8,128)(2,1)} %inter_hbm.1, ...), custom_call_target="tpu_custom_call" | custom-call | tf_op jit(solution)/shard_map/pallas_call | solution.py:623
  27.4 0.8 %shard_map.105 = (f32[4,128,128]{2,1,0:T(8,128)}, f32[4,128,128]{2,1,0:T(8,128)}) custom-call(f32[4,128,128]{2,1,0:T(8,128)S(1)} %get-tuple-element.4.amps, f32[4,128,128]{2,1,0:T(8,128)S(1)} %get-tuple-element.5.dressed), custom_call_target="tpu_custom_call" | custom-call | tf_op jit(solution)/shard_map/pallas_call | solution.py:683

commit v6 on v5

--- a/solution.py
+++ b/solution.py
@@ -73,10 +73,6 @@
     part_send,
     part_recv,
     relay_recv,
-    inter_sem,
-    maps_sem,
-    orb_sem,
-    small_sem,
 ):
     own_pairs = amps_hbm.shape[0]
     orbs = orb_hbm.shape[0]
@@ -143,7 +139,7 @@
             )
 
     small_copies = [
-        pltpu.make_async_copy(source_ref, target_ref, small_sem.at[at])
+        pltpu.make_async_copy(source_ref, target_ref, amp_recv.at[ITERS - 1, at])
         for at, (source_ref, target_ref) in enumerate(
             (
                 (amps_hbm, amplitudes),
@@ -429,7 +425,7 @@
                     out_amps[i] = values[i]
 
     win_start(0, True)
-    orb_copy = pltpu.make_async_copy(orb_hbm, window.at[0, middle], orb_sem)
+    orb_copy = pltpu.make_async_copy(orb_hbm, window.at[0, middle], relay_recv.at[ITERS - 1, 0])
     orb_copy.start()
     small_copies[0].wait()
     for i in range(own_pairs):
@@ -437,9 +433,9 @@
     amps_start(0, range(own_pairs))
     for copy in small_copies[1:]:
         copy.start()
-    maps_copy = pltpu.make_async_copy(maps_hbm, maps, maps_sem)
+    maps_copy = pltpu.make_async_copy(maps_hbm, maps, part_recv.at[ITERS - 1, 0])
     maps_copy.start()
-    inter_copy = pltpu.make_async_copy(inter_hbm, inter, inter_sem)
+    inter_copy = pltpu.make_async_copy(inter_hbm, inter, part_recv.at[ITERS - 1, 1])
     inter_copy.start()
 
     for copy in small_copies[1:]:
@@ -659,10 +655,6 @@
             dma((ITERS,)),
             dma((ITERS, own_pairs // BATCH)),
             dma((ITERS, own_pairs // BATCH)),
-            dma,
-            dma,
-            dma,
-            dma((6,)),
         ],
         compiler_params=pltpu.CompilerParams(
             collective_id=0, has_side_effects=True, vmem_limit_bytes=67043328 - 4096 * 1024

time: 28.4 us -> 28.3 us (level)
  no operation moved by 1% of the time
where the time goes in v6:
time: 28.3 us; the launch traced here: 28.1 us
  Pallas kernels  27.5 us (97%)
  between operations  0.64 us (2%)
    pallas_call x1, Pallas kernels, on_device(): pl.pallas_call(functools.partial(kernel, ranks, groups), out_shape=(pltpu...  26.7 us
    pallas_call x1, Pallas kernels, on_device(): pl.pallas_call(store, out_shape=tuple((pltpu.HBM(x.shape, x.dtype) for x...  0.81 us

profile of v6, /device:TPU:0, one launch (start us, length us, event | category | flops | bytes accessed | tf_op | source)
XLA Modules:
  0.0 28.1 jit_solution(6335518016277973379)
XLA Ops:
  0.6 26.7 %shard_map.104 = (f32[4,128,128]{2,1,0:T(8,128)S(1)}, f32[4,128,128]{2,1,0:T(8,128)S(1)}) custom-call(s32[4,16]{1,0:T(4,128)} %couple_hbm.1, s32[16]{0:T(128)} %first_hbm.1, s32[16]{0:T(128)} %second_hbm.1, f32[32]{0:T(128)} %energy_hbm.1, f32[4,128,128]{2,1,0:T(8,128)} %amps_hbm.1, f32[4,128]{1,0:T(4,128)} %pno_hbm.1, bf16[4,16,128,128]{3,2,1,0:T(8,128)(2,1)} %inter_hbm.1, ...), custom_call_target="tpu_custom_call" | custom-call | tf_op jit(solution)/shard_map/pallas_call | solution.py:619
  27.3 0.8 %shard_map.105 = (f32[4,128,128]{2,1,0:T(8,128)}, f32[4,128,128]{2,1,0:T(8,128)}) custom-call(f32[4,128,128]{2,1,0:T(8,128)S(1)} %get-tuple-element.4.amps, f32[4,128,128]{2,1,0:T(8,128)S(1)} %get-tuple-element.5.dressed), custom_call_target="tpu_custom_call" | custom-call | tf_op jit(solution)/shard_map/pallas_call | solution.py:675

commit v7 on v5

--- a/solution.py
+++ b/solution.py
@@ -13,6 +13,8 @@
 
 dress_scale = 0.015
 BATCH = 2
+GATHER_FAR = "none"
+FORWARD_EARLY = False
 SUM_DIRECT = ("outer", "none")
 NONE = ("none", "none")
 FIRST_RELAY = "all"
@@ -174,6 +176,8 @@
     def amp_slot(step, i):
         if not square:
             return step
+        if step == 3:
+            return own_pairs + 1
         return i if relayed_tile(step, i) else own_pairs
 
     def amp_copy(turn, step, i):
@@ -198,10 +202,16 @@
             device_id_type=pl.DeviceIdType.MESH,
         )
 
-    def relay_all(turn):
-        for i in range(own_pairs):
+    def relay_some(turn, some):
+        for i in some:
             amp_copy(turn, 1 if i % 2 == 0 else 2, i).wait_recv()
             amp_relay(turn, i).start()
+
+    def relay_all(turn):
+        relay_some(turn, range(own_pairs))
+
+    beyond = range(BATCH, own_pairs)
+    direct_far = {"all": True, "outer": jnp.logical_not(inner), "none": False}[GATHER_FAR]
 
     def amp_wait(turn, slot):
         block = amps.at[turn, pl.ds(own, own_pairs)]
@@ -275,8 +285,15 @@
         for step in range(ranks - 1, 0, -1):
             amp_copy(turn, step, i).start()
 
-    def amps_start(turn, batch):
+    def amps_start(turn, batch, later=False):
         if square:
+            if later and batch[0] >= BATCH:
+
+                def far():
+                    for i in batch:
+                        amp_copy(turn, 3, i).start()
+
+                either(direct_far, far, nothing)
             for turned in (0, 1):
                 for i in batch:
                     amp_copy(turn, 1 if (i + turned) % 2 == 0 else 2, i).start()
@@ -421,7 +438,7 @@
             def _(batch=batch, values=values):
                 for i in batch:
                     amps[turn + 1, own + i] = values[i].astype(bf16)
-                amps_start(turn + 1, batch)
+                amps_start(turn + 1, batch, True)
 
             @pl.when(turn + 1 == ITERS)
             def _(batch=batch, values=values):
@@ -529,8 +546,17 @@
             def _():
                 sums(turn, 0)
                 throughs(turn, (0,))
-                relay_all(turn)
+                relay_some(turn, range(BATCH))
+                either(direct_far, nothing, lambda: relay_some(turn, beyond))
                 sums(turn, 1)
+                if FORWARD_EARLY:
+                    either(inner, nothing, lambda: forward_all(turn))
+
+                def late():
+                    for i in beyond:
+                        amp_copy(turn, 1 if i % 2 == 0 else 2, i).wait_recv()
+
+                either(direct_far, late, nothing)
 
             if EARLY_NEAR:
 
@@ -546,13 +572,18 @@
             def _():
                 throughs(turn, (0,))
 
+        if square and not FORWARD_EARLY:
+
+            @pl.when(jnp.logical_and(turn > 0, jnp.logical_not(inner)))
+            def _():
+                forward_all(turn)
+
         fit_near(turn)
         if square:
 
             @pl.when(turn > 0)
             def _():
                 sums(turn, 2)
-                either(inner, nothing, lambda: forward_all(turn))
 
         throughs(turn, far_steps)
         dress(turn)

time: 28.4 us -> 28.3 us (level)
  no operation moved by 1% of the time
where the time goes in v7:
time: 28.3 us; the launch traced here: 28.2 us
  Pallas kernels  27.5 us (97%)
  between operations  0.64 us (2%)
    pallas_call x1, Pallas kernels, on_device(): pl.pallas_call(functools.partial(kernel, ranks, groups), out_shape=(pltpu...  26.7 us
    pallas_call x1, Pallas kernels, on_device(): pl.pallas_call(store, out_shape=tuple((pltpu.HBM(x.shape, x.dtype) for x...  0.81 us

profile of v7, /device:TPU:0, one launch (start us, length us, event | category | flops | bytes accessed | tf_op | source)
XLA Modules:
  0.0 28.2 jit_solution(18247047074244946954)
XLA Ops:
  0.6 26.7 %shard_map.104 = (f32[4,128,128]{2,1,0:T(8,128)S(1)}, f32[4,128,128]{2,1,0:T(8,128)S(1)}) custom-call(s32[4,16]{1,0:T(4,128)} %couple_hbm.1, s32[16]{0:T(128)} %first_hbm.1, s32[16]{0:T(128)} %second_hbm.1, f32[32]{0:T(128)} %energy_hbm.1, f32[4,128,128]{2,1,0:T(8,128)} %amps_hbm.1, f32[4,128]{1,0:T(4,128)} %pno_hbm.1, bf16[4,16,128,128]{3,2,1,0:T(8,128)(2,1)} %inter_hbm.1, ...), custom_call_target="tpu_custom_call" | custom-call | tf_op jit(solution)/shard_map/pallas_call | solution.py:654
  27.3 0.8 %shard_map.105 = (f32[4,128,128]{2,1,0:T(8,128)}, f32[4,128,128]{2,1,0:T(8,128)}) custom-call(f32[4,128,128]{2,1,0:T(8,128)S(1)} %get-tuple-element.4.amps, f32[4,128,128]{2,1,0:T(8,128)S(1)} %get-tuple-element.5.dressed), custom_call_target="tpu_custom_call" | custom-call | tf_op jit(solution)/shard_map/pallas_call | solution.py:714
